TPU v7x, 32 devices: a whole 2x2x4 slice. The times are simulated.
32 devices in a mesh: groups: 2 (over x), dom: 16 (over z, y, core).
Axes of the slice: x: 2, y: 2, z: 4, core: 2. Of those that a mesh axis runs over, the one named last changes fastest.
Arguments:
- particles: bfloat16 [1024, 4096], P(('groups', 'dom')), parts along dimension 0, may hold values from -5 to 5
- dataset: bfloat16 [2048, 4096], P(('groups', 'dom')), parts along dimension 0, may hold values from -0.09375 to 0.09375
- labels: int32 [2048], P(('groups', 'dom')), parts along dimension 0, may hold values 0 or 1
- batch_index: int32 [512], P(('groups', 'dom')), parts along dimension 0, may hold values from 0 to 1023, as said below
Outputs:
- driving: float32 [1024, 4096], P(('groups', 'dom')), parts along dimension 0
- spreading: float32 [1024, 4096], P(('groups', 'dom')), parts along dimension 0
There are 2 independent parts, one for each index of `groups`. A program takes and returns all parts, laid end to end along the dimension named above; each array names one. Nothing has to cross between parts.
Inputs may be any that keep to these rules, and one draw needn't show every extreme that they name: `batch_index`: entry b names a row of block b // 16 of the dataset, that is a row from (b // 16) * 64 to (b // 16 + 1) * 64 - 1; rows may repeat.
All inputs are finite; a program needn't handle non-finite values. No bound on the sum of `labels` on one device may be relied on, other than what follows from the above.
Results may differ from a plain program's by a relative error of at most 0.0003.
Values may be sent and summed in bfloat16 or wider, within the bound.
A program may use at most 128 MiB of HBM per device.

v0:
```python
import jax
import jax.numpy as jnp
from jax import lax
from jax.sharding import PartitionSpec as P

D = 4096


prior_precision = 1.0


def per_device(particles, dataset, labels, batch_index):
    own_rows = dataset.shape[0]
    local_index = batch_index - lax.axis_index("dom") * own_rows
    rows = jnp.take(dataset, local_index, axis=0)
    targets = jnp.take(labels, local_index).astype(jnp.bfloat16)
    particles_f = particles.astype(jnp.float32)
    ratio = float(own_rows) / float(batch_index.shape[0])
    all_rows, all_targets = (
        lax.all_gather(rows, "dom", axis=0, tiled=True),
        lax.all_gather(targets, "dom", axis=0, tiled=True),
    )
    logits = lax.dot_general(
        particles, all_rows, (((1,), (1,)), ((), ())), preferred_element_type=jnp.float32
    )
    misfit = (all_targets.astype(jnp.float32)[None, :] - jax.nn.sigmoid(logits)).astype(
        jnp.bfloat16
    )
    pulled = jnp.dot(misfit, all_rows, preferred_element_type=jnp.float32)
    scores = (-prior_precision * particles_f + ratio * pulled).astype(jnp.bfloat16)
    squares = jnp.sum(particles_f * particles_f, axis=1)
    kernel_scale = 0.25 * D
    others = lax.all_gather(particles, "dom", axis=0, tiled=True)
    other_scores = lax.all_gather(scores, "dom", axis=0, tiled=True)
    others_f = others.astype(jnp.float32)
    other_squares = jnp.sum(others_f * others_f, axis=1)
    cross = lax.dot_general(
        particles, others, (((1,), (1,)), ((), ())), preferred_element_type=jnp.float32
    )
    dist = squares[:, None] + other_squares[None, :] - 2.0 * cross
    kernel = jnp.exp(-dist / kernel_scale)
    kernel_b = kernel.astype(jnp.bfloat16)
    drive = jnp.dot(kernel_b, other_scores, preferred_element_type=jnp.float32)
    pull = jnp.dot(kernel_b, others, preferred_element_type=jnp.float32)
    rowsum = jnp.sum(kernel, axis=1)
    drive, pull, rowsum = (drive, pull, rowsum)
    total = float(particles.shape[0] * lax.axis_size("dom"))
    driving = drive / total
    spreading = (particles_f * rowsum[:, None] - pull) / total
    return (driving, spreading)


def solution(mesh):
    placed = (
        P(("groups", "dom"), None),
        P(("groups", "dom"), None),
        P(("groups", "dom")),
        P(("groups", "dom")),
    )
    return jax.shard_map(
        per_device,
        mesh=mesh,
        in_specs=placed,
        out_specs=(P(("groups", "dom"), None), P(("groups", "dom"), None)),
        check_vma=False,
    )
```

profile of v0, /device:TPU:0, one launch (start us, length us, event | category | flops | bytes accessed | tf_op | source)
XLA Modules:
  0.0 168.4 jit_solution(8589020766125148358)
XLA Ops:
  7.2 0.0 copy-start
  7.2 0.0 copy-start.2
  7.2 0.0 all-gather.6.cloned.1.call-start
  7.2 0.7 compare_and_fusion
  8.0 0.3 copy-done
  8.2 0.6 gather_fusion.1
  8.9 0.7 broadcast_select_fusion
  9.6 0.0 all-gather.6.cloned.1.call-update
  9.6 0.0 all-gather.4.cloned.1.call-start
  9.7 0.7 all-gather.4.cloned.1.call-update
  10.4 0.0 all-gather.8.cloned.1.call-start
  10.4 1.3 gather_fusion
  11.7 1.2 dynamic-slice
  13.7 0.2 dynamic-update-slice
  13.9 35.2 %all-reduce = bf16[256]{0:T(256)(128)(2,1)S(1)} all-reduce(bf16[256]{0:T(256)(128)(2,1)S(1)} %dynamic-update-slice), channel_id=1, replica_groups=mesh['groups'=2,'dom'=16] {'dom'}, use_global_device_ids=true, to_apply=%add | all-reduce | flops 256 | bytes 1024
  49.1 5.8 %all-gather.6.cloned.1.call-done = bf16[256,4096]{1,0:T(8,128)(2,1)} async-done(((bf16[16,4096]{1,0:T(8,128)(2,1)}), bf16[256,4096]{1,0:T(8,128)(2,1)}) %all-gather.6.cloned.1.call-update) | async-done | bytes 2097168 | tf_op jit(solution)/shard_map/all_gather | solution.py:20
  55.0 4.6 %fusion.2 = bf16[32,4096]{1,0:T(8,128)(2,1)} fusion(bf16[256,4096]{1,0:T(8,128)(2,1)} %all-gather.6.cloned.1.call-done, bf16[32,4096]{1,0:T(8,128)(2,1)} %param.4, f32[256]{0:T(256)S(1)} %convert_element_type.25), kind=kOutput, calls=%fused_computation.8 | convolution fusion | flops 134914048 | bytes 2622464 | tf_op jit(solution)/shard_map/dot_general | solution.py:29
  59.6 0.0 all-gather.8.cloned.1.call-update
  59.7 0.0 copy-done.2
  59.7 0.2 fusion.12
  59.8 46.5 %all-gather.4.cloned.1.call-done = bf16[512,4096]{1,0:T(8,128)(2,1)} async-done(((bf16[32,4096]{1,0:T(8,128)(2,1)}), bf16[512,4096]{1,0:T(8,128)(2,1)}) %all-gather.4.cloned.1.call-update) | async-done | bytes 4194320 | tf_op jit(solution)/shard_map/all_gather | solution.py:33
  106.4 0.0 copy-start.1
  106.4 3.2 %multiply_reduce_fusion = f32[512]{0:T(512)S(1)} fusion(bf16[512,4096]{1,0:T(8,128)(2,1)} %all-gather.4.cloned.1.call-done), kind=kLoop, calls=%fused_computation.2 | loop fusion | flops 6290944 | bytes 4196352 | tf_op jit(solution)/shard_map/reduce_sum | solution.py:36
  109.6 0.2 copy-done.1
  109.8 1.5 fusion.18
  111.3 1.6 fusion
  112.9 45.1 %all-gather.8.cloned.1.call-done = bf16[512,4096]{1,0:T(8,128)(2,1)} async-done(((bf16[32,4096]{1,0:T(8,128)(2,1)}), bf16[512,4096]{1,0:T(8,128)(2,1)}) %all-gather.8.cloned.1.call-update) | async-done | bytes 4194320 | tf_op jit(solution)/shard_map/all_gather | solution.py:34
  158.0 3.8 %convolution_multiply_fusion = f32[32,4096]{1,0:T(8,128)} fusion(bf16[512,4096]{1,0:T(8,128)(2,1)} %all-gather.8.cloned.1.call-done, bf16[32,512]{1,0:T(8,128)(2,1)S(1)} %get-tuple-element.5), kind=kOutput, calls=%fused_computation.5 | convolution fusion | flops 134348800 | bytes 4751360 | tf_op jit(solution)/shard_map/dot_general | solution.py:43
  (4 shorter events, 0.0 us)
Async XLA Ops:
  7.2 1.1 copy-start
  7.2 52.5 %copy-start.2 = (bf16[32,4096]{1,0:T(8,128)(2,1)S(1)}, bf16[32,4096]{1,0:T(8,128)(2,1)}, u32[]{:S(2)}) copy-start(bf16[32,4096]{1,0:T(8,128)(2,1)} %param.4) | copy-start | bytes 786436
  7.2 47.8 %all-gather.6.cloned.1.call-start = ((), (), s32[]{:S(2)}) async-start(), calls=%async_computation.1 | async-start | bytes 2228224 | tf_op jit(solution)/shard_map/all_gather | solution.py:20
  9.6 96.7 %all-gather.4.cloned.1.call-start = ((), (), s32[]{:S(2)}) async-start(), calls=%async_computation | async-start | bytes 4456448 | tf_op jit(solution)/shard_map/all_gather | solution.py:33
  10.4 147.7 %all-gather.8.cloned.1.call-start = ((), (), s32[]{:S(2)}) async-start(), calls=%async_computation.2 | async-start | bytes 4456448 | tf_op jit(solution)/shard_map/all_gather | solution.py:34
  106.4 3.4 %copy-start.1 = (bf16[512,4096]{1,0:T(8,128)(2,1)S(1)}, bf16[512,4096]{1,0:T(8,128)(2,1)}, u32[]{:S(2)}) copy-start(bf16[512,4096]{1,0:T(8,128)(2,1)} %all-gather.4.cloned.1.call-done) | copy-start | bytes 12582916
Sparse Core Ops, SparseCore 0:
  10.7 44.2 all-gather.5
  57.1 49.1 all-gather.3
  109.1 48.9 all-gather.7
where the time goes:
time: 169 us; the launch traced here: 168 us
  waiting for transfers between devices  98.2 us (58%)
  blocking collectives  35.2 us (21%)
  between operations  14.5 us (9%)
  matrix products  11.6 us (7%)
  other arithmetic  4.88 us (3%)
  local copies, waits for them, and re-layouts  3.92 us (2%)
    all_gather x1, waiting for transfers between devices, per_device(): others = lax.all_gather(particles, 'dom', axis=0, tiled=True)  46.5 us
    all_gather x1, waiting for transfers between devices, per_device(): other_scores = lax.all_gather(scores, 'dom', axis=0, tiled=True)  45.1 us
    unnamed x1, blocking collectives  35.2 us
    all_gather x1, waiting for transfers between devices, per_device(): lax.all_gather(rows, 'dom', axis=0, tiled=True)  5.83 us
    dot_general x1, matrix products, per_device(): pulled = jnp.dot(misfit, all_rows, preferred_element_type=jnp.float32)  4.65 us
    dot_general x1, matrix products, per_device(): drive = jnp.dot(kernel_b, other_scores, preferred_element_type=jnp.float32)  3.81 us
  transfers between devices with their start and end apart: 3, of which 3 were waited for; matrix products, arithmetic and copies ran while one was open for 8% of the time, Pallas kernels for 0%

commit v1 on v0

v1 whole, which is shorter than its diff:
```python
import functools

import jax
import jax.numpy as jnp
from jax import lax
from jax.experimental import pallas as pl
from jax.experimental.pallas import tpu as pltpu
from jax.sharding import PartitionSpec as P

prior_precision = 1.0
MESH = pl.DeviceIdType.MESH
CROSS = 512
TILE = 512


class Stream:
    def __init__(self, buf, splits, recv, up, down, side, core):
        self.buf, self.splits, self.recv = buf, splits, recv
        self.sems = {"up": up, "down": down, "side": side, "core": core}


def kernel(n, particles, dataset, labels, index, drive_out, spread_out,
           held, rows, drive, pull, rowsum, target_row, own_sq, local_sem, *sems):
    planes = n // 4
    d = particles.shape[1]
    batch = rows.shape[0] * rows.shape[1]
    group = 4 * particles.shape[0]
    own_rows = dataset.shape[0]
    ratio = float(own_rows) / float(rows.shape[1])
    inv_scale = 1.0 / (0.25 * d)
    total = float(particles.shape[0] * n)

    me = lax.axis_index("dom")
    core = me % 2
    y = (me // 2) % 2
    z = me // 4
    target = {"up": me + 4, "down": me - 4, "side": me + 2 - 4 * y, "core": me + 1 - 2 * core}
    has_up, has_down = z < planes - 1, z > 0
    row_stream = Stream(rows, ((0, d - CROSS), (d - CROSS, CROSS + 128)), *sems[:5])
    part_stream = Stream(held, ((0, d - CROSS), (d - CROSS, CROSS)), *sems[5:])

    def block_of(p, yy, cc):
        return (p * 2 + yy) * 2 + cc

    def copy(st, k, b, way):
        view = st.buf.at[b, :, pl.ds(*st.splits[k])]
        return pltpu.make_async_remote_copy(
            src_ref=view, dst_ref=view, send_sem=st.sems[way].at[k, b], recv_sem=st.recv.at[k, b],
            device_id={"dom": target[way]}, device_id_type=MESH)

    def send(st, k, b, way, go):
        c = copy(st, k, b, way)
        c.start() if go else c.wait_send()

    def arrived(st, k, b):
        copy(st, k, b, "core").wait_recv()

    def own(st, go):
        for k in (1, 0):
            send(st, k, me, "side", go)

            @pl.when(has_up)
            def _():
                send(st, k, me, "up", go)

            @pl.when(has_down)
            def _():
                send(st, k, me, "down", go)

            send(st, k, me, "core", go)

    def own_cross(st, go):
        b = target["side"]
        if go:
            arrived(st, 1, b)

        @pl.when(has_up)
        def _():
            send(st, 1, b, "up", go)

        @pl.when(has_down)
        def _():
            send(st, 1, b, "down", go)

        send(st, 1, b, "core", go)

    def relay(st, p, go):
        for k, b, crosses in ((1, block_of(p, y, core), False), (0, block_of(p, y, core), True),
                              (1, block_of(p, 1 - y, core), False)):
            if go:
                arrived(st, k, b)

            @pl.when(jnp.logical_and(p > z, has_down))
            def _():
                send(st, k, b, "down", go)

            @pl.when(jnp.logical_and(p < z, has_up))
            def _():
                send(st, k, b, "up", go)

            if crosses:
                send(st, k, b, "side", go)
            send(st, k, b, "core", go)

    def finish_side(st, p, go):
        b = block_of(p, 1 - y, core)
        if go:
            arrived(st, 0, b)
        send(st, 0, b, "core", go)

    def finish_core(st, p):
        for yy in (0, 1):
            for k in (1, 0):
                arrived(st, k, block_of(p, yy, 1 - core))

    near = jnp.minimum(z, planes - 1 - z)
    outward = jnp.where(z <= planes - 1 - z, 1, -1)

    def distance(q):
        return jnp.where(q <= 2 * near, (q + 1) // 2, q - near)

    def plane(q):
        two_sided = jnp.where(q % 2 == 1, -1, 1)
        return z + jnp.where(q <= 2 * near, two_sided, outward) * distance(q)

    def within(s):
        return jnp.minimum(z, s) + jnp.minimum(planes - 1 - z, s) + 1

    def each(lo, hi, f):
        lax.fori_loop(lo, hi, lambda q, x: (f(plane(q)), x)[1], 0)

    load = pltpu.make_async_copy(particles, held.at[me], local_sem)
    load.start()
    barrier = pltpu.get_barrier_semaphore()

    def greet(way):
        pl.semaphore_signal(barrier, inc=1, device_id={"dom": target[way]}, device_id_type=MESH)

    greet("core")
    greet("side")
    pl.when(has_up)(lambda: greet("up"))
    pl.when(has_down)(lambda: greet("down"))

    m = rows.shape[1]
    square = (m, m)
    diagonal = lax.broadcasted_iota(jnp.int32, square, 0) == lax.broadcasted_iota(jnp.int32, square, 1)
    local = (index[...] - me * own_rows).astype(jnp.float32)
    wanted = jnp.sum(jnp.where(diagonal, jnp.broadcast_to(local, square), 0.0), axis=1, keepdims=True)
    pick = lax.broadcasted_iota(jnp.int32, (m, own_rows), 1).astype(jnp.float32) == wanted
    targets = jnp.sum(jnp.where(pick, jnp.broadcast_to(labels[...].astype(jnp.float32), pick.shape), 0.0),
                      axis=1, keepdims=True)
    pick_b = pick.astype(jnp.float32).astype(jnp.bfloat16)
    rows[me, :, pl.ds(d, 128)] = jnp.broadcast_to(targets, (m, 128)).astype(jnp.bfloat16)
    for t in range(0, d, TILE):
        rows[me, :, pl.ds(t, TILE)] = jnp.dot(
            pick_b, dataset[:, pl.ds(t, TILE)], preferred_element_type=jnp.float32).astype(jnp.bfloat16)

    pl.semaphore_wait(barrier, 2 + has_up.astype(jnp.int32) + has_down.astype(jnp.int32))

    own(row_stream, True)
    own_cross(row_stream, True)
    each(1, planes, lambda p: relay(row_stream, p, True))
    load.wait()
    own(part_stream, True)
    each(0, planes, lambda p: finish_side(row_stream, p, True))
    own_cross(part_stream, True)
    each(0, planes, lambda p: finish_core(row_stream, p))

    drive[...] = jnp.zeros_like(drive)
    pull[...] = jnp.zeros_like(pull)
    rowsum[...] = jnp.zeros_like(rowsum)
    labels_in = rows[:, :, pl.ds(d, 128)].reshape(batch, 128).astype(jnp.float32)
    target_row[...] = jnp.transpose(labels_in)[0:8, :]
    own_f = held[me].astype(jnp.float32)
    own_sq[...] = jnp.broadcast_to(jnp.sum(own_f * own_f, axis=1, keepdims=True), own_sq.shape)

    def columns(t):
        return pl.ds(pl.multiple_of(t * TILE, TILE), TILE)

    def absorb(p):
        first = p * 4

        def measure(t, sums):
            logits, cross, sq = sums
            part = held[pl.ds(first, 4), :, columns(t)].reshape(group, TILE)
            feat = rows[:, :, columns(t)].reshape(batch, TILE)
            mine = held[me, :, columns(t)]
            nt = (((1,), (1,)), ((), ()))
            logits += lax.dot_general(part, feat, nt, preferred_element_type=jnp.float32)
            cross += lax.dot_general(mine, part, nt, preferred_element_type=jnp.float32)
            part_f = part.astype(jnp.float32)
            part_f = part_f * part_f
            for i in range(0, TILE, 128):
                sq += part_f[:, i:i + 128]
            return logits, cross, sq

        logits, cross, sq = lax.fori_loop(0, d // TILE, measure, (
            jnp.zeros((group, batch), jnp.float32), jnp.zeros((particles.shape[0], group), jnp.float32),
            jnp.zeros((group, 128), jnp.float32)))
        misfit = (target_row[0:1, :] - jax.nn.sigmoid(logits)).astype(jnp.bfloat16)
        sq = jnp.transpose(jnp.broadcast_to(jnp.sum(sq, axis=1, keepdims=True), (group, 128)))[0:1, :]
        dist = own_sq[:, 0:1] + sq - 2.0 * cross
        weight = jnp.exp(-dist * inv_scale)
        rowsum[...] += jnp.broadcast_to(jnp.sum(weight, axis=1, keepdims=True), rowsum.shape)
        weight_b = weight.astype(jnp.bfloat16)

        @pl.loop(0, d // TILE)
        def _(t):
            part = held[pl.ds(first, 4), :, columns(t)].reshape(group, TILE)
            feat = rows[:, :, columns(t)].reshape(batch, TILE)
            pulled = jnp.dot(misfit, feat, preferred_element_type=jnp.float32)
            score = (ratio * pulled - prior_precision * part.astype(jnp.float32)).astype(jnp.bfloat16)
            drive[:, columns(t)] += jnp.dot(weight_b, score, preferred_element_type=jnp.float32)
            pull[:, columns(t)] += jnp.dot(weight_b, part, preferred_element_type=jnp.float32)

    def step(q, done):
        p = plane(q)
        ready = jnp.minimum(within(distance(q) + 1), planes)
        each(done, ready, lambda r: relay(part_stream, r, True))
        finish_side(part_stream, p, True)
        finish_core(part_stream, p)
        absorb(p)
        return ready

    lax.fori_loop(0, planes, step, jnp.int32(1))

    drive_out[...] = drive[...] / total
    spread_out[...] = (held[me].astype(jnp.float32) * rowsum[:, 0:1] - pull[...]) / total

    for st in (row_stream, part_stream):
        own(st, False)
        own_cross(st, False)
        each(1, planes, functools.partial(relay, st, go=False))
        each(0, planes, functools.partial(finish_side, st, go=False))


def per_device(particles, dataset, labels, batch_index):
    n = lax.axis_size("dom")
    k, d = particles.shape
    m = batch_index.shape[0]
    vmem = pl.BlockSpec(memory_space=pltpu.VMEM)
    sems = [pltpu.SemaphoreType.DMA((2, n))] * 10
    out = jax.ShapeDtypeStruct((k, d), jnp.float32)
    return pl.pallas_call(
        functools.partial(kernel, n),
        out_shape=(out, out),
        in_specs=[pl.BlockSpec(memory_space=pl.ANY), vmem, vmem, vmem],
        out_specs=(vmem, vmem),
        scratch_shapes=[
            pltpu.VMEM((n, k, d), jnp.bfloat16),
            pltpu.VMEM((n, m, d + 128), jnp.bfloat16),
            pltpu.VMEM((k, d), jnp.float32),
            pltpu.VMEM((k, d), jnp.float32),
            pltpu.VMEM((k, 128), jnp.float32),
            pltpu.VMEM((8, n * m), jnp.float32),
            pltpu.VMEM((k, 128), jnp.float32),
            pltpu.SemaphoreType.DMA,
        ] + sems,
        compiler_params=pltpu.CompilerParams(
            collective_id=0, has_side_effects=True, vmem_limit_bytes=56 * 1024 * 1024),
    )(particles, dataset, labels[None, :], batch_index[None, :])


def solution(mesh):
    whole = P(("groups", "dom"), None)
    return jax.shard_map(
        per_device,
        mesh=mesh,
        in_specs=(whole, whole, P(("groups", "dom")), P(("groups", "dom"))),
        out_specs=(whole, whole),
        check_vma=False,
    )
```

time: 169 us -> 61.7 us (0.37)
  waiting for transfers between devices: 98.2 us -> 0 us
  Pallas kernels: 0 us -> 58.2 us
  blocking collectives: 35.2 us -> 0 us
  between operations: 14.5 us -> 0.65 us
  matrix products: 11.6 us -> 0 us
  other arithmetic: 4.88 us -> 0 us
    all_gather x3 -> x0, waiting for transfers between devices: 97.5 us -> none  [the longest x1 46.5 us: per_device(): others = lax.all_gather(particles, 'dom', axis=0, tiled=True)]
    pallas_call x0 -> x1, Pallas kernels: none -> 58.2 us  [per_device(): pl.pallas_call(functools.partial(kernel, n), out_shape=(out, out), in_spe...]
    unnamed x1 -> x0, blocking collectives: 35.2 us -> none
    dot_general x4 -> x0, matrix products: 11.6 us -> none  [the longest x1 4.65 us: per_device(): pulled = jnp.dot(misfit, all_rows, preferred_element_type=jnp.float32)]
    reduce_sum x2 -> x0, other arithmetic: 3.4 us -> none  [the longest x1 3.23 us: per_device(): other_squares = jnp.sum(others_f * others_f, axis=1)]
    gather x2 -> x0, local copies, waits for them, and re-layouts: 1.94 us -> none  [the longest x1 1.32 us: per_device(): targets = jnp.take(labels, local_index).astype(jnp.bfloat16)]
  transfers between devices with their start and end apart: 3 -> 0, of which waited for: 3 -> 0; matrix products, arithmetic and copies ran while one was open for 8% -> 0% of each run, Pallas kernels for 0% -> 0%
where the time goes in v1:
time: 61.7 us; the launch traced here: 61.6 us
  Pallas kernels  58.2 us (94%)
  local copies, waits for them, and re-layouts  2.72 us (4%)
  between operations  0.65 us (1%)
    pallas_call x1, Pallas kernels, per_device(): pl.pallas_call(functools.partial(kernel, n), out_shape=(out, out), in_spe...  58.2 us
    unnamed x4, local copies, waits for them, and re-layouts  2.72 us

profile of v1, /device:TPU:0, one launch (start us, length us, event | category | flops | bytes accessed | tf_op | source)
XLA Modules:
  0.0 61.6 jit_solution(13720341045805871309)
XLA Ops:
  0.6 58.2 %shard_map.59 = (f32[32,4096]{1,0:T(8,128)}, f32[32,4096]{1,0:T(8,128)}) custom-call(bf16[32,4096]{1,0:T(8,128)(2,1)} %particles.1, bf16[64,4096]{1,0:T(8,128)(2,1)} %dataset.1, s32[1,64]{1,0:T(1,128)} %bitcast.2, s32[1,16]{1,0:T(1,128)} %bitcast.3), custom_call_target="tpu_custom_call" | custom-call | tf_op jit(solution)/shard_map/pallas_call | solution.py:244
  58.8 0.0 copy-start
  58.8 1.9 %copy.8 = f32[32,4096]{1,0:T(8,128)} copy(f32[32,4096]{1,0:T(8,128)} %get-tuple-element.4) | data formatting | bytes 1048576
  60.8 0.0 copy-done
  60.8 0.8 %copy.9 = f32[32,4096]{1,0:T(8,128)} copy(f32[32,4096]{1,0:T(8,128)S(1)} %copy-done) | data formatting | bytes 1048576
Async XLA Ops:
  58.8 1.9 %copy-start = (f32[32,4096]{1,0:T(8,128)S(1)}, f32[32,4096]{1,0:T(8,128)}, u32[]{:S(2)}) copy-start(f32[32,4096]{1,0:T(8,128)} %get-tuple-element.5) | copy-start | bytes 1572868

commit v2 on v1

v2 whole, which is shorter than its diff:
```python
import functools

import jax
import jax.numpy as jnp
from jax import lax
from jax.experimental import pallas as pl
from jax.experimental.pallas import tpu as pltpu
from jax.sharding import PartitionSpec as P

prior_precision = 1.0
MESH = pl.DeviceIdType.MESH
CROSS = 512
PIECES = 1
TILE = 512
MEASURE = 4096
APPLY = 4096


def cut(d, extra):
    step = -(-(d - CROSS) // (PIECES * TILE)) * TILE
    starts = list(range(0, d - CROSS, step))
    return [(a, min(step, d - CROSS - a)) for a in starts] + [(d - CROSS, CROSS + extra)]


class Stream:
    def __init__(self, buf, splits, recv, up, down, side, core):
        self.buf, self.splits, self.recv = buf, splits, recv
        self.sems = {"up": up, "down": down, "side": side, "core": core}


def kernel(n, particles, dataset, labels, index, drive_out, spread_out,
           held, rows, drive, pull, rowsum, target_row, own_sq, data, local_sem, data_sem, *sems):
    planes = n // 4
    d = particles.shape[1]
    batch = rows.shape[0] * rows.shape[1]
    group = 4 * particles.shape[0]
    own_rows = dataset.shape[0]
    ratio = float(own_rows) / float(rows.shape[1])
    inv_scale = 1.0 / (0.25 * d)
    total = float(particles.shape[0] * n)

    me = lax.axis_index("dom")
    core = me % 2
    y = (me // 2) % 2
    z = me // 4
    target = {"up": me + 4, "down": me - 4, "side": me + 2 - 4 * y, "core": me + 1 - 2 * core}
    has_up, has_down = z < planes - 1, z > 0
    row_stream = Stream(rows, cut(d, 128), *sems[:5])
    part_stream = Stream(held, cut(d, 0), *sems[5:])
    last = len(row_stream.splits) - 1
    main = range(last)

    def block_of(p, yy, cc):
        return (p * 2 + yy) * 2 + cc

    def copy(st, k, b, way):
        view = st.buf.at[b, :, pl.ds(*st.splits[k])]
        return pltpu.make_async_remote_copy(
            src_ref=view, dst_ref=view, send_sem=st.sems[way].at[k, b], recv_sem=st.recv.at[k, b],
            device_id={"dom": target[way]}, device_id_type=MESH)

    def send(st, k, b, way, go):
        c = copy(st, k, b, way)
        c.start() if go else c.wait_send()

    def arrived(st, k, b):
        copy(st, k, b, "core").wait_recv()

    def own_column(st, way, go):
        for k in range(last + 1):
            send(st, k, me, way, go)

    def own_side(st, go):
        for k in main:
            send(st, k, me, "side", go)

    def own_core(st, go):
        for k in range(last + 1):
            send(st, k, me, "core", go)

    def own_cross(st, go):
        b = target["side"]
        if go:
            arrived(st, last, b)

        @pl.when(has_up)
        def _():
            send(st, last, b, "up", go)

        @pl.when(has_down)
        def _():
            send(st, last, b, "down", go)

        send(st, last, b, "core", go)

    def relay(st, s, go):
        def one(valid, p, onward, way, k, across):
            @pl.when(valid)
            def _():
                b = block_of(p, 1 - y if across else y, core)
                if go:
                    arrived(st, k, b)

                @pl.when(onward)
                def _():
                    send(st, k, b, way, go)

                if k < last:
                    send(st, k, b, "side", go)
                send(st, k, b, "core", go)

        for k, across in [(k, False) for k in range(last + 1)] + [(last, True)]:
            one(z - s >= 0, z - s, has_up, "up", k, across)
            one(z + s < planes, z + s, has_down, "down", k, across)

    def side_piece(st, k, p, go):
        b = block_of(p, 1 - y, core)
        if go:
            arrived(st, k, b)
        send(st, k, b, "core", go)

    def finish_side(st, p, go):
        for k in main:
            side_piece(st, k, p, go)

    def core_piece(st, k, p):
        for yy in (0, 1):
            arrived(st, k, block_of(p, yy, 1 - core))

    def finish_core(st, p):
        for k in range(last + 1):
            core_piece(st, k, p)

    near = jnp.minimum(z, planes - 1 - z)
    outward = jnp.where(z <= planes - 1 - z, 1, -1)

    def distance(q):
        return jnp.where(q <= 2 * near, (q + 1) // 2, q - near)

    def plane(q):
        two_sided = jnp.where(q % 2 == 1, -1, 1)
        return z + jnp.where(q <= 2 * near, two_sided, outward) * distance(q)

    reach = jnp.maximum(z, planes - 1 - z)

    def each(lo, hi, f):
        lax.fori_loop(lo, hi, lambda q, x: (f(plane(q)), x)[1], 0)

    load = pltpu.make_async_copy(particles, held.at[me], local_sem)
    fetch = pltpu.make_async_copy(dataset, data, data_sem)
    fetch.start()
    load.start()
    barrier = pltpu.get_barrier_semaphore()

    def greet(way):
        pl.semaphore_signal(barrier, inc=1, device_id={"dom": target[way]}, device_id_type=MESH)

    greet("core")
    greet("side")
    pl.when(has_up)(lambda: greet("up"))
    pl.when(has_down)(lambda: greet("down"))

    m = rows.shape[1]
    square = (m, m)
    diagonal = lax.broadcasted_iota(jnp.int32, square, 0) == lax.broadcasted_iota(jnp.int32, square, 1)
    local = (index[...] - me * own_rows).astype(jnp.float32)
    wanted = jnp.sum(jnp.where(diagonal, jnp.broadcast_to(local, square), 0.0), axis=1, keepdims=True)
    pick = lax.broadcasted_iota(jnp.int32, (m, own_rows), 1).astype(jnp.float32) == wanted
    targets = jnp.sum(jnp.where(pick, jnp.broadcast_to(labels[...].astype(jnp.float32), pick.shape), 0.0),
                      axis=1, keepdims=True)
    pick_b = pick.astype(jnp.float32).astype(jnp.bfloat16)
    rows[me, :, pl.ds(d, 128)] = jnp.broadcast_to(targets, (m, 128)).astype(jnp.bfloat16)
    fetch.wait()
    for t in range(0, d, TILE):
        rows[me, :, pl.ds(t, TILE)] = jnp.dot(
            pick_b, data[:, pl.ds(t, TILE)], preferred_element_type=jnp.float32).astype(jnp.bfloat16)

    pl.semaphore_wait(barrier, 2 + has_up.astype(jnp.int32) + has_down.astype(jnp.int32))

    def column(st, cond, way, go):
        pl.when(cond)(lambda: own_column(st, way, go))

    send(row_stream, last, me, "side", True)
    own_side(row_stream, True)
    column(row_stream, has_up, "up", True)
    column(row_stream, has_down, "down", True)
    own_core(row_stream, True)
    load.wait()
    send(part_stream, last, me, "side", True)
    own_core(part_stream, True)
    own_cross(row_stream, True)
    column(part_stream, z == 0, "up", True)
    column(part_stream, z == planes - 1, "down", True)

    def relay_rows(s, x):
        relay(row_stream, s, True)
        column(part_stream, jnp.logical_and(s == z, has_up), "up", True)
        column(part_stream, jnp.logical_and(s == planes - 1 - z, has_down), "down", True)
        return x

    lax.fori_loop(1, reach + 1, relay_rows, 0)
    own_side(part_stream, True)
    each(0, planes, lambda p: finish_side(row_stream, p, True))
    own_cross(part_stream, True)
    each(0, planes, lambda p: finish_core(row_stream, p))

    drive[...] = jnp.zeros_like(drive)
    pull[...] = jnp.zeros_like(pull)
    rowsum[...] = jnp.zeros_like(rowsum)
    labels_in = rows[:, :, pl.ds(d, 128)].reshape(batch, 128).astype(jnp.float32)
    target_row[...] = jnp.transpose(labels_in)[0:8, :]
    own_f = held[me].astype(jnp.float32)
    own_sq[...] = jnp.broadcast_to(jnp.sum(own_f * own_f, axis=1, keepdims=True), own_sq.shape)

    def columns(t, width):
        return pl.ds(pl.multiple_of(t * width, width), width)

    def absorb(p):
        first = p * 4

        def measure(t, sums):
            logits, cross, sq = sums
            part = held[pl.ds(first, 4), :, columns(t, MEASURE)].reshape(group, MEASURE)
            feat = rows[:, :, columns(t, MEASURE)].reshape(batch, MEASURE)
            mine = held[me, :, columns(t, MEASURE)]
            nt = (((1,), (1,)), ((), ()))
            logits += lax.dot_general(part, feat, nt, preferred_element_type=jnp.float32)
            cross += lax.dot_general(mine, part, nt, preferred_element_type=jnp.float32)
            part_f = part.astype(jnp.float32)
            part_f = part_f * part_f
            for i in range(0, MEASURE, 128):
                sq += part_f[:, i:i + 128]
            return logits, cross, sq

        sums = (jnp.zeros((group, batch), jnp.float32), jnp.zeros((particles.shape[0], group), jnp.float32),
                jnp.zeros((group, 128), jnp.float32))
        finish_side(part_stream, p, True)
        finish_core(part_stream, p)
        logits, cross, sq = lax.fori_loop(0, d // MEASURE, measure, sums)
        misfit = (target_row[0:1, :] - jax.nn.sigmoid(logits)).astype(jnp.bfloat16)
        sq = jnp.transpose(jnp.broadcast_to(jnp.sum(sq, axis=1, keepdims=True), (group, 128)))[0:1, :]
        dist = own_sq[:, 0:1] + sq - 2.0 * cross
        weight = jnp.exp(-dist * inv_scale)
        rowsum[...] += jnp.broadcast_to(jnp.sum(weight, axis=1, keepdims=True), rowsum.shape)
        weight_b = weight.astype(jnp.bfloat16)

        @pl.loop(0, d // APPLY)
        def _(t):
            part = held[pl.ds(first, 4), :, columns(t, APPLY)].reshape(group, APPLY)
            feat = rows[:, :, columns(t, APPLY)].reshape(batch, APPLY)
            pulled = jnp.dot(misfit, feat, preferred_element_type=jnp.float32)
            score = (ratio * pulled - prior_precision * part.astype(jnp.float32)).astype(jnp.bfloat16)
            drive[:, columns(t, APPLY)] += jnp.dot(weight_b, score, preferred_element_type=jnp.float32)
            pull[:, columns(t, APPLY)] += jnp.dot(weight_b, part, preferred_element_type=jnp.float32)

    def pass_on(lo, hi, go):
        lax.fori_loop(lo, hi, lambda s, x: (relay(part_stream, s, go), x)[1], 0)

    def step(q, done):
        p = plane(q)
        ready = jnp.minimum(distance(q) + 1, reach) + 1
        pass_on(done, ready, True)
        absorb(p)
        return ready

    def settle(st, until):
        send(st, last, me, "side", False)
        own_side(st, False)
        own_core(st, False)
        column(st, has_up, "up", False)
        column(st, has_down, "down", False)
        own_cross(st, False)
        each(0, until, functools.partial(finish_side, st, go=False))

    done = lax.fori_loop(0, planes - 1, step, jnp.int32(1))
    settle(row_stream, planes)
    lax.fori_loop(1, reach + 1, lambda s, x: (relay(row_stream, s, False), x)[1], 0)
    settle(part_stream, planes - 1)
    step(planes - 1, done)

    drive_out[...] = drive[...] / total
    spread_out[...] = (held[me].astype(jnp.float32) * rowsum[:, 0:1] - pull[...]) / total

    finish_side(part_stream, plane(planes - 1), False)
    pass_on(1, reach + 1, False)


def per_device(particles, dataset, labels, batch_index):
    n = lax.axis_size("dom")
    k, d = particles.shape
    m = batch_index.shape[0]
    vmem = pl.BlockSpec(memory_space=pltpu.VMEM)
    sems = [pltpu.SemaphoreType.DMA((len(cut(d, 0)), n))] * 10

    out = jax.ShapeDtypeStruct((k, d), jnp.float32)
    return pl.pallas_call(
        functools.partial(kernel, n),
        out_shape=(out, out),
        in_specs=[pl.BlockSpec(memory_space=pltpu.HBM)] * 2 + [vmem] * 2,
        out_specs=(vmem, vmem),
        scratch_shapes=[
            pltpu.VMEM((n, k, d), jnp.bfloat16),
            pltpu.VMEM((n, m, d + 128), jnp.bfloat16),
            pltpu.VMEM((k, d), jnp.float32),
            pltpu.VMEM((k, d), jnp.float32),
            pltpu.VMEM((k, 128), jnp.float32),
            pltpu.VMEM((8, n * m), jnp.float32),
            pltpu.VMEM((k, 128), jnp.float32),
            pltpu.VMEM(dataset.shape, jnp.bfloat16),
            pltpu.SemaphoreType.DMA,
            pltpu.SemaphoreType.DMA,
        ] + sems,
        compiler_params=pltpu.CompilerParams(
            collective_id=0, has_side_effects=True, vmem_limit_bytes=56 * 1024 * 1024),
    )(particles, dataset, labels[None, :], batch_index[None, :])


def solution(mesh):
    whole = P(("groups", "dom"), None)
    return jax.shard_map(
        per_device,
        mesh=mesh,
        in_specs=(whole, whole, P(("groups", "dom")), P(("groups", "dom"))),
        out_specs=(whole, whole),
        check_vma=False,
    )
```

time: 61.7 us -> 53 us (0.86)
  Pallas kernels: 58.2 us -> 49.4 us
    pallas_call x1, Pallas kernels: 58.2 us -> 49.4 us  [per_device(): pl.pallas_call(functools.partial(kernel, n), out_shape=(out, out), in_spe...]
where the time goes in v2:
time: 53 us; the launch traced here: 52.8 us
  Pallas kernels  49.4 us (93%)
  local copies, waits for them, and re-layouts  2.72 us (5%)
  between operations  0.65 us (1%)
    pallas_call x1, Pallas kernels, per_device(): pl.pallas_call(functools.partial(kernel, n), out_shape=(out, out), in_spe...  49.4 us
    unnamed x4, local copies, waits for them, and re-layouts  2.72 us

profile of v2, /device:TPU:0, one launch (start us, length us, event | category | flops | bytes accessed | tf_op | source)
XLA Modules:
  0.0 52.8 jit_solution(13249343415985100931)
XLA Ops:
  0.6 49.4 %shard_map.59 = (f32[32,4096]{1,0:T(8,128)}, f32[32,4096]{1,0:T(8,128)}) custom-call(bf16[32,4096]{1,0:T(8,128)(2,1)} %particles.1, bf16[64,4096]{1,0:T(8,128)(2,1)} %dataset.1, s32[1,64]{1,0:T(1,128)} %bitcast.2, s32[1,16]{1,0:T(1,128)} %bitcast.3), custom_call_target="tpu_custom_call" | custom-call | tf_op jit(solution)/shard_map/pallas_call | solution.py:296
  50.1 0.0 copy-start
  50.1 1.9 %copy.8 = f32[32,4096]{1,0:T(8,128)} copy(f32[32,4096]{1,0:T(8,128)} %get-tuple-element.4) | data formatting | bytes 1048576
  52.0 0.0 copy-done
  52.0 0.8 %copy.9 = f32[32,4096]{1,0:T(8,128)} copy(f32[32,4096]{1,0:T(8,128)S(1)} %copy-done) | data formatting | bytes 1048576
Async XLA Ops:
  50.1 1.9 %copy-start = (f32[32,4096]{1,0:T(8,128)S(1)}, f32[32,4096]{1,0:T(8,128)}, u32[]{:S(2)}) copy-start(f32[32,4096]{1,0:T(8,128)} %get-tuple-element.5) | copy-start | bytes 1572868

commit v3 on v2

--- a/solution.py
+++ b/solution.py
@@ -10,14 +10,12 @@
 prior_precision = 1.0
 MESH = pl.DeviceIdType.MESH
 CROSS = 512
-PIECES = 1
+PIECES = 2
 TILE = 512
-MEASURE = 4096
-APPLY = 4096
 
 
 def cut(d, extra):
-    step = -(-(d - CROSS) // (PIECES * TILE)) * TILE
+    step = -(-(d - CROSS) // (PIECES * 128)) * 128
     starts = list(range(0, d - CROSS, step))
     return [(a, min(step, d - CROSS - a)) for a in starts] + [(d - CROSS, CROSS + extra)]
 
@@ -212,46 +210,29 @@
     own_f = held[me].astype(jnp.float32)
     own_sq[...] = jnp.broadcast_to(jnp.sum(own_f * own_f, axis=1, keepdims=True), own_sq.shape)
 
-    def columns(t, width):
-        return pl.ds(pl.multiple_of(t * width, width), width)
-
     def absorb(p):
         first = p * 4
 
-        def measure(t, sums):
-            logits, cross, sq = sums
-            part = held[pl.ds(first, 4), :, columns(t, MEASURE)].reshape(group, MEASURE)
-            feat = rows[:, :, columns(t, MEASURE)].reshape(batch, MEASURE)
-            mine = held[me, :, columns(t, MEASURE)]
-            nt = (((1,), (1,)), ((), ()))
-            logits += lax.dot_general(part, feat, nt, preferred_element_type=jnp.float32)
-            cross += lax.dot_general(mine, part, nt, preferred_element_type=jnp.float32)
-            part_f = part.astype(jnp.float32)
-            part_f = part_f * part_f
-            for i in range(0, MEASURE, 128):
-                sq += part_f[:, i:i + 128]
-            return logits, cross, sq
-
-        sums = (jnp.zeros((group, batch), jnp.float32), jnp.zeros((particles.shape[0], group), jnp.float32),
-                jnp.zeros((group, 128), jnp.float32))
         finish_side(part_stream, p, True)
         finish_core(part_stream, p)
-        logits, cross, sq = lax.fori_loop(0, d // MEASURE, measure, sums)
+        part = held[pl.ds(first, 4)].reshape(group, d)
+        feat = rows[:, :, pl.ds(0, d)].reshape(batch, d)
+        nt = (((1,), (1,)), ((), ()))
+        logits = lax.dot_general(part, feat, nt, preferred_element_type=jnp.float32)
+        cross = lax.dot_general(held[me], part, nt, preferred_element_type=jnp.float32)
+        part_f = part.astype(jnp.float32)
+        sq = jnp.sum(part_f * part_f, axis=1, keepdims=True)
         misfit = (target_row[0:1, :] - jax.nn.sigmoid(logits)).astype(jnp.bfloat16)
-        sq = jnp.transpose(jnp.broadcast_to(jnp.sum(sq, axis=1, keepdims=True), (group, 128)))[0:1, :]
+        sq = jnp.transpose(jnp.broadcast_to(sq, (group, 128)))[0:1, :]
         dist = own_sq[:, 0:1] + sq - 2.0 * cross
         weight = jnp.exp(-dist * inv_scale)
         rowsum[...] += jnp.broadcast_to(jnp.sum(weight, axis=1, keepdims=True), rowsum.shape)
         weight_b = weight.astype(jnp.bfloat16)
 
-        @pl.loop(0, d // APPLY)
-        def _(t):
-            part = held[pl.ds(first, 4), :, columns(t, APPLY)].reshape(group, APPLY)
-            feat = rows[:, :, columns(t, APPLY)].reshape(batch, APPLY)
-            pulled = jnp.dot(misfit, feat, preferred_element_type=jnp.float32)
-            score = (ratio * pulled - prior_precision * part.astype(jnp.float32)).astype(jnp.bfloat16)
-            drive[:, columns(t, APPLY)] += jnp.dot(weight_b, score, preferred_element_type=jnp.float32)
-            pull[:, columns(t, APPLY)] += jnp.dot(weight_b, part, preferred_element_type=jnp.float32)
+        pulled = jnp.dot(misfit, feat, preferred_element_type=jnp.float32)
+        score = (ratio * pulled - prior_precision * part_f).astype(jnp.bfloat16)
+        drive[...] += jnp.dot(weight_b, score, preferred_element_type=jnp.float32)
+        pull[...] += jnp.dot(weight_b, part, preferred_element_type=jnp.float32)
 
     def pass_on(lo, hi, go):
         lax.fori_loop(lo, hi, lambda s, x: (relay(part_stream, s, go), x)[1], 0)

time: 53 us -> 51.9 us (0.979)
  Pallas kernels: 49.4 us -> 48.4 us
    pallas_call x1, Pallas kernels: 49.4 us -> 48.4 us  [per_device(): pl.pallas_call(functools.partial(kernel, n), out_shape=(out, out), in_spe...]
where the time goes in v3:
time: 51.9 us; the launch traced here: 51.7 us
  Pallas kernels  48.4 us (93%)
  local copies, waits for them, and re-layouts  2.72 us (5%)
  between operations  0.65 us (1%)
    pallas_call x1, Pallas kernels, per_device(): pl.pallas_call(functools.partial(kernel, n), out_shape=(out, out), in_spe...  48.4 us
    unnamed x4, local copies, waits for them, and re-layouts  2.72 us

profile of v3, /device:TPU:0, one launch (start us, length us, event | category | flops | bytes accessed | tf_op | source)
XLA Modules:
  0.0 51.7 jit_solution(816571162699669497)
XLA Ops:
  0.6 48.4 %shard_map.59 = (f32[32,4096]{1,0:T(8,128)}, f32[32,4096]{1,0:T(8,128)}) custom-call(bf16[32,4096]{1,0:T(8,128)(2,1)} %particles.1, bf16[64,4096]{1,0:T(8,128)(2,1)} %dataset.1, s32[1,64]{1,0:T(1,128)} %bitcast.2, s32[1,16]{1,0:T(1,128)} %bitcast.3), custom_call_target="tpu_custom_call" | custom-call | tf_op jit(solution)/shard_map/pallas_call | solution.py:277
  49.0 0.0 copy-start
  49.0 1.9 %copy.8 = f32[32,4096]{1,0:T(8,128)} copy(f32[32,4096]{1,0:T(8,128)} %get-tuple-element.4) | data formatting | bytes 1048576
  50.9 0.0 copy-done
  50.9 0.8 %copy.9 = f32[32,4096]{1,0:T(8,128)} copy(f32[32,4096]{1,0:T(8,128)S(1)} %copy-done) | data formatting | bytes 1048576
Async XLA Ops:
  49.0 1.9 %copy-start = (f32[32,4096]{1,0:T(8,128)S(1)}, f32[32,4096]{1,0:T(8,128)}, u32[]{:S(2)}) copy-start(f32[32,4096]{1,0:T(8,128)} %get-tuple-element.5) | copy-start | bytes 1572868

commit v4 on v3

--- a/solution.py
+++ b/solution.py
@@ -292,7 +292,7 @@
             pltpu.SemaphoreType.DMA,
         ] + sems,
         compiler_params=pltpu.CompilerParams(
-            collective_id=0, has_side_effects=True, vmem_limit_bytes=56 * 1024 * 1024),
+            collective_id=0, has_side_effects=True, vmem_limit_bytes=53500 * 1024),
     )(particles, dataset, labels[None, :], batch_index[None, :])
 
 

time: 51.9 us -> 50.8 us (0.979)
  Pallas kernels: 48.4 us -> 46.7 us
    pallas_call x1, Pallas kernels: 48.4 us -> 46.7 us  [per_device(): pl.pallas_call(functools.partial(kernel, n), out_shape=(out, out), in_spe...]
    unnamed x4 -> x8, local copies, waits for them, and re-layouts: 2.72 us -> 3.19 us
where the time goes in v4:
time: 50.8 us; the launch traced here: 50.6 us
  Pallas kernels  46.7 us (92%)
  local copies, waits for them, and re-layouts  3.19 us (6%)
  between operations  0.66 us (1%)
    pallas_call x1, Pallas kernels, per_device(): pl.pallas_call(functools.partial(kernel, n), out_shape=(out, out), in_spe...  46.7 us
    unnamed x8, local copies, waits for them, and re-layouts  3.19 us

profile of v4, /device:TPU:0, one launch (start us, length us, event | category | flops | bytes accessed | tf_op | source)
XLA Modules:
  0.0 50.6 jit_solution(2939768577025822765)
XLA Ops:
  0.6 0.0 copy-start.1
  0.6 0.0 copy-start.2
  0.7 0.6 %copy-done.1 = s32[64]{0:T(128)S(1)} copy-done((s32[64]{0:T(128)S(1)}, s32[64]{0:T(128)}, u32[]{:S(2)}) %copy-start.1) | copy-done | bytes 280
  1.3 0.0 copy-done.2
  1.3 0.0 copy-start
  1.3 0.9 %copy-done = bf16[32,4096]{1,0:T(8,128)(2,1)S(1)} copy-done((bf16[32,4096]{1,0:T(8,128)(2,1)S(1)}, bf16[32,4096]{1,0:T(8,128)(2,1)}, u32[]{:S(2)}) %copy-start) | copy-done | bytes 262168
  2.3 46.7 %shard_map.59 = (f32[32,4096]{1,0:T(8,128)S(1)}, f32[32,4096]{1,0:T(8,128)S(1)}) custom-call(bf16[32,4096]{1,0:T(8,128)(2,1)S(1)} %copy-done, bf16[64,4096]{1,0:T(8,128)(2,1)} %dataset.1, s32[1,64]{1,0:T(1,128)S(1)} %bitcast.2, s32[1,16]{1,0:T(1,128)S(1)} %bitcast.3), custom_call_target="tpu_custom_call" | custom-call | tf_op jit(solution)/shard_map/pallas_call | solution.py:277
  49.0 0.8 %copy.8 = f32[32,4096]{1,0:T(8,128)} copy(f32[32,4096]{1,0:T(8,128)S(1)} %get-tuple-element.4) | data formatting | bytes 1048576
  49.8 0.8 %copy.9 = f32[32,4096]{1,0:T(8,128)} copy(f32[32,4096]{1,0:T(8,128)S(1)} %get-tuple-element.5) | data formatting | bytes 1048576
Async XLA Ops:
  0.6 0.7 %copy-start.1 = (s32[64]{0:T(128)S(1)}, s32[64]{0:T(128)}, u32[]{:S(2)}) copy-start(s32[64]{0:T(128)} %param.6) | copy-start | bytes 772
  0.6 0.7 %copy-start.2 = (s32[16]{0:T(128)S(1)}, s32[16]{0:T(128)}, u32[]{:S(2)}) copy-start(s32[16]{0:T(128)} %param.7) | copy-start | bytes 196
  1.3 0.9 %copy-start = (bf16[32,4096]{1,0:T(8,128)(2,1)S(1)}, bf16[32,4096]{1,0:T(8,128)(2,1)}, u32[]{:S(2)}) copy-start(bf16[32,4096]{1,0:T(8,128)(2,1)} %particles.1) | copy-start | bytes 786436
